TPU v7x, 32 devices: a whole 2x2x4 slice. The times are simulated.
32 devices in a mesh: fsdp: 4 (over y, x), rep: 8 (over z, core).
Axes of the slice: x: 2, y: 2, z: 4, core: 2. Of those that a mesh axis runs over, the one named last changes fastest.
Arguments:
- hidden_in: bfloat16 [8192, 2048], P(('fsdp', 'rep'))
- out_grad: bfloat16 [8192, 2048], P(('fsdp', 'rep')), may hold values from -6 to 6
- attn_saved: bfloat16 [8192, 256], P(('fsdp', 'rep')), may hold values from -6 to 6
- row_lse: float32 [8192, 2], P(('fsdp', 'rep')), may hold values from 2.5 to 6
- w_qkv: bfloat16 [2048, 512], P('fsdp'), may hold values from -0.125 to 0.125
- w_out_t: bfloat16 [2048, 256], P('fsdp'), may hold values from -0.125 to 0.125
- doc_lengths: int32 [32, 4], P(('fsdp', 'rep')), may hold values from 1 to 128, 256 in all within a row
- seq_start: int32 [32], P(('fsdp', 'rep')), may hold values from 0 to 2047
Outputs:
- input_grad: bfloat16 [8192, 2048], P(('fsdp', 'rep'))
- grad_update: float32 [2048, 768], P('fsdp')
- grad_norm: float32 [], replicated
Inputs may be any that keep to these rules, and one draw needn't show every extreme that they name: `doc_lengths`: each row sums to 256; the longest document of each device has exactly 128 tokens.
All inputs are finite; a program needn't handle non-finite values.
Results may differ from a plain program's by a relative error of at most 0.014.
Values may be sent and summed in bfloat16 or wider, within the bound.
A program may use at most 64 MiB of HBM per device.

v0:
```python
import jax
import jax.numpy as jnp
from jax import lax
from jax.sharding import PartitionSpec as P

D = 2048
HEAD = 128


def rotary(values_in, positions, turn, head_size):
    rows = values_in.shape[0]
    heads_count = values_in.shape[1] // head_size
    half_size = head_size // 2
    inverse = 1000000.0 ** (-(jnp.arange(half_size, dtype=jnp.float32) * 2.0) / head_size)
    angles = positions.astype(jnp.float32)[:, None] * inverse[None, :]
    cosine = jnp.cos(angles)[:, None, :]
    sines = jnp.sin(angles)[:, None, :]
    shaped = values_in.reshape(rows, heads_count, head_size)
    first_half = shaped[:, :, :half_size]
    second_half = shaped[:, :, half_size:]
    result = jnp.concatenate(
        [
            first_half * cosine - turn * second_half * sines,
            second_half * cosine + turn * first_half * sines,
        ],
        axis=2,
    )
    return result.reshape(rows, heads_count * head_size)


def contract_rows(left, right):
    return lax.dot_general(
        left, right, (((0,), (0,)), ((), ())), preferred_element_type=jnp.float32
    )


def contract_cols(left, right):
    return lax.dot_general(
        left, right, (((1,), (1,)), ((), ())), preferred_element_type=jnp.float32
    )


def body(hidden_in, out_grad, attn_saved, row_lse, w_qkv, w_out_t, doc_lengths, seq_start):
    seq_rows = hidden_in.shape[0]
    head_size = HEAD
    query_width = attn_saved.shape[1]
    heads_count = row_lse.shape[1]
    scale = 1.0 / head_size**0.5
    tokens_part = hidden_in
    grads_part = out_grad
    proj = jnp.dot(
        tokens_part,
        lax.all_gather(w_qkv, "fsdp", axis=0, tiled=True),
        preferred_element_type=jnp.float32,
    )
    attn_full = jnp.dot(
        grads_part,
        lax.all_gather(w_out_t, "fsdp", axis=0, tiled=True),
        preferred_element_type=jnp.float32,
    )
    attn_grad = attn_full.astype(jnp.bfloat16)
    positions = seq_start[0] + jnp.arange(seq_rows, dtype=jnp.int32)
    queries = rotary(proj[:, :query_width], positions, 1.0, head_size).astype(jnp.bfloat16)
    keys = rotary(proj[:, query_width : query_width + head_size], positions, 1.0, head_size).astype(
        jnp.bfloat16
    )
    values_all = proj[:, query_width + head_size :].astype(jnp.bfloat16)
    ends = jnp.cumsum(doc_lengths[0])
    local_rows = jnp.arange(seq_rows, dtype=jnp.int32)
    documents = jnp.sum((local_rows[:, None] >= ends[None, :]).astype(jnp.int32), axis=1)
    block_rows = min(seq_rows, 512)
    block_count = seq_rows // block_rows

    def attend_block(carry, inputs):
        key_grad, value_grad = carry
        query_rows, grad_rows, saved_rows, lse_rows, index_rows, doc_rows = inputs
        allowed = (doc_rows[:, None] == documents[None, :]) & (
            local_rows[None, :] <= index_rows[:, None]
        )
        query_parts = []
        for head_index in range(heads_count):
            lower = head_index * head_size
            query_head = query_rows[:, lower : lower + head_size]
            scores = contract_cols(query_head, keys) * scale
            probs = jnp.where(
                allowed, jnp.exp(scores - lse_rows[:, head_index : head_index + 1]), 0.0
            )
            grad_head = grad_rows[:, lower : lower + head_size]
            dprobs = contract_cols(grad_head, values_all)
            delta = jnp.sum(
                grad_head.astype(jnp.float32)
                * saved_rows[:, lower : lower + head_size].astype(jnp.float32),
                axis=1,
                keepdims=True,
            )
            dscores = (probs * (dprobs - delta) * scale).astype(jnp.bfloat16)
            probs_low = probs.astype(jnp.bfloat16)
            value_grad = value_grad + contract_rows(probs_low, grad_head)
            query_parts.append(jnp.dot(dscores, keys, preferred_element_type=jnp.float32))
            key_grad = key_grad + contract_rows(dscores, query_head)
        return ((key_grad, value_grad), jnp.concatenate(query_parts, axis=1))

    block_inputs = (
        queries.reshape(block_count, block_rows, query_width),
        attn_grad.reshape(block_count, block_rows, query_width),
        attn_saved.reshape(block_count, block_rows, query_width),
        row_lse.reshape(block_count, block_rows, heads_count),
        local_rows.reshape(block_count, block_rows),
        documents.reshape(block_count, block_rows),
    )
    zero_grad = jnp.zeros((seq_rows, head_size), jnp.float32)
    (key_grad, value_grad), query_blocks = lax.scan(
        attend_block, (zero_grad, zero_grad), block_inputs
    )
    query_grad = rotary(
        query_blocks.reshape(seq_rows, query_width), positions, -1.0, head_size
    ).astype(jnp.bfloat16)
    key_grad = rotary(key_grad, positions, -1.0, head_size).astype(jnp.bfloat16)
    d_qkv = jnp.concatenate([query_grad, key_grad, value_grad.astype(jnp.bfloat16)], axis=1)
    input_full = contract_cols(d_qkv, lax.all_gather(w_qkv, "fsdp", axis=0, tiled=True))
    input_grad = input_full.astype(jnp.bfloat16)
    tokens_part = hidden_in
    grads_part = out_grad
    shard_sum = lax.psum_scatter(
        jnp.concatenate(
            [contract_rows(tokens_part, d_qkv), contract_rows(grads_part, attn_saved)], axis=1
        ).astype(jnp.bfloat16),
        "fsdp",
        scatter_dimension=0,
        tiled=True,
    ).astype(jnp.float32)
    grads = lax.psum(shard_sum, "rep")
    norm_sq = lax.psum(jnp.sum(grads * grads), "fsdp")
    grad_update = grads * lax.rsqrt(norm_sq / (D * grads.shape[1]) + 1e-06)
    return (input_grad, grad_update, jnp.sqrt(norm_sq))


def solution(mesh):
    in_specs = (
        P(("fsdp", "rep"), None),
        P(("fsdp", "rep"), None),
        P(("fsdp", "rep"), None),
        P(("fsdp", "rep"), None),
        P("fsdp", None),
        P("fsdp", None),
        P(("fsdp", "rep"), None),
        P(("fsdp", "rep")),
    )
    out_specs = (P(("fsdp", "rep"), None), P("fsdp", None), P())
    return jax.shard_map(body, mesh=mesh, in_specs=in_specs, out_specs=out_specs, check_vma=False)
```

profile of v0, /device:TPU:0, one launch (start us, length us, event | category | flops | bytes accessed | tf_op | source)
XLA Modules:
  0.0 219.8 jit_solution(17886597577698370556)
XLA Ops:
  9.4 0.9 fusion.49
  10.3 0.7 copy.36
  11.0 0.7 copy.37
  11.7 0.8 reduce-window.8
  13.2 1.3 fusion.50
  14.6 1.2 broadcast_multiply_fusion.1
  15.8 1.4 convolution_convert_fusion.2
  17.2 21.9 %all-gather.5.cloned.1.call-done = bf16[2048,256]{1,0:T(8,128)(2,1)} async-done(((bf16[512,256]{1,0:T(8,128)(2,1)}), bf16[2048,256]{1,0:T(8,128)(2,1)}) %all-gather.5.cloned.1.call-update) | async-done | bytes 1048592 | tf_op jit(solution)/shard_map/all_gather | solution.py:58
  39.1 1.7 convolution_convert_fusion.3
  40.8 0.9 multiply_reduce_fusion.1
  41.8 34.4 %all-gather.3.cloned.1.call-done = bf16[2048,512]{1,0:T(8,128)(2,1)} async-done(((bf16[512,512]{1,0:T(8,128)(2,1)}), bf16[2048,512]{1,0:T(8,128)(2,1)}) %all-gather.3.cloned.1.call-update) | async-done | bytes 2097168 | tf_op jit(solution)/shard_map/all_gather | solution.py:53
  76.1 2.3 %fusion.51 = f32[256,512]{1,0:T(8,128)S(1)} fusion(bf16[256,2048]{1,0:T(8,128)(2,1)S(1)} %copy-done, bf16[2048,512]{1,0:T(8,128)(2,1)} %all-gather.3.cloned.1.call-done), kind=kOutput, calls=%fused_computation.89 | convolution fusion | flops 536870912 | bytes 3670016 | tf_op jit(solution)/shard_map/dot_general | solution.py:51
  78.6 1.0 fusion.28
  80.6 1.0 fusion.10
  84.4 1.2 subtract_convert_fusion
  86.0 0.7 fusion
  86.7 1.9 pad_maximum_fusion
  88.7 44.1 %reduce-scatter.2.cloned.1.call-done = bf16[512,768]{0,1:T(8,128)(2,1)} async-done(((bf16[2048,768]{0,1:T(8,128)(2,1)}), bf16[512,768]{0,1:T(8,128)(2,1)}) %reduce-scatter.2.cloned.1.call-update) | async-done | bytes 786448 | tf_op jit(solution)/shard_map/reduce_scatter | solution.py:124
  132.7 59.9 %all-reduce.1 = f32[512,768]{0,1:T(8,128)S(1)} all-reduce(bf16[512,768]{0,1:T(8,128)(2,1)} %reduce-scatter.2.cloned.1.call-done), channel_id=1, replica_groups=mesh['fsdp'=4,'rep'=8] {'rep'}, use_global_device_ids=true, to_apply=%region_5.6 | all-reduce | flops 393216 | bytes 2359296 | tf_op jit(solution)/shard_map/psum | solution.py:132
  192.6 1.0 multiply_reduce_fusion
  193.6 3.3 %convolution_convert_fusion.1 = bf16[256,2048]{1,0:T(8,128)(2,1)} fusion(bf16[2048,512]{1,0:T(8,128)(2,1)} %all-gather.3.cloned.1.call-done, bf16[256,128]{1,0:T(8,128)(2,1)S(1)} %copy.33, bf16[256,128]{1,0:T(8,128)(2,1)S(1)} %copy.32, bf16[256,256]{1,0:T(8,128)(2,1)S(1)} %bitcast.49), kind=kOutput, calls=%fused_computation.3 | convolution fusion | flops 538181632 | bytes 3407872 | tf_op jit(solution)/shard_map/dot_general | solution.py:38
  196.9 9.5 %psum.15 = f32[]{:T(128)} all-reduce(f32[]{:T(128)} %multiply_reduce_fusion), channel_id=1, replica_groups=mesh['fsdp'=4,'rep'=8] {'fsdp'}, use_global_device_ids=true, to_apply=%region_7.8 | all-reduce | flops 1 | bytes 8 | tf_op jit(solution)/shard_map/psum | solution.py:133
  207.8 1.3 broadcast_multiply_fusion
  209.1 3.0 %copy.34 = f32[512,768]{1,0:T(8,128)} copy(f32[512,768]{0,1:T(8,128)} %broadcast_multiply_fusion) | data formatting | bytes 3145728
  (47 shorter events, 6.4 us)
Async XLA Ops:
  7.2 69.0 %copy-start = (bf16[256,2048]{1,0:T(8,128)(2,1)S(1)}, bf16[256,2048]{1,0:T(8,128)(2,1)}, u32[]{:S(2)}) copy-start(bf16[256,2048]{1,0:T(8,128)(2,1)} %param.8) | copy-start | bytes 3145732
  7.2 8.6 %copy-start.1 = (bf16[256,2048]{1,0:T(8,128)(2,1)S(1)}, bf16[256,2048]{1,0:T(8,128)(2,1)}, u32[]{:S(2)}) copy-start(bf16[256,2048]{1,0:T(8,128)(2,1)} %param.9) | copy-start | bytes 3145732
  7.2 31.9 %all-gather.5.cloned.1.call-start = ((), (), s32[]{:S(2)}) async-start(), calls=%async_computation.2 | async-start | bytes 1310720 | tf_op jit(solution)/shard_map/all_gather | solution.py:58
  7.9 68.2 %all-gather.3.cloned.1.call-start = ((), (), s32[]{:S(2)}) async-start(), calls=%async_computation.1 | async-start | bytes 2621440 | tf_op jit(solution)/shard_map/all_gather | solution.py:53
  8.7 124.0 %reduce-scatter.2.cloned.1.call-start = ((), (), s32[]{:S(2)}) async-start(), calls=%async_computation.3 | async-start | bytes 3932160 | tf_op jit(solution)/shard_map/reduce_scatter | solution.py:124
  79.7 2.3 %copy-start.2 = (bf16[256,1,64]{0,2,1:T(8,128)(2,1)S(1)}, bf16[256,1,64]{0,2,1:T(8,128)(2,1)}, u32[]{:S(2)}) copy-start(bf16[256,1,64]{0,2,1:T(8,128)(2,1)} %get-tuple-element.64) | copy-start | bytes 98308
  79.7 2.3 %copy-start.3 = (bf16[256,1,64]{0,2,1:T(8,128)(2,1)S(1)}, bf16[256,1,64]{0,2,1:T(8,128)(2,1)}, u32[]{:S(2)}) copy-start(bf16[256,1,64]{0,2,1:T(8,128)(2,1)} %get-tuple-element.65) | copy-start | bytes 98308
  79.7 2.7 %copy-start.4 = (f32[256,1]{0,1:T(1,128)S(1)}, f32[256,1]{0,1:T(1,128)}, u32[]{:S(2)}) copy-start(f32[256,1]{0,1:T(1,128)} %get-tuple-element.68) | copy-start | bytes 3076
  79.7 2.7 %copy-start.5 = (s32[256]{0:T(256)S(1)}, s32[256]{0:T(256)}, u32[]{:S(2)}) copy-start(s32[256]{0:T(256)} %convert_reduce_fusion) | copy-start | bytes 3076
Sparse Core Ops, SparseCore 0:
  9.8 29.2 all-gather.4
  40.9 35.1 all-gather.2
  88.8 43.8 reduce-scatter.1
where the time goes:
time: 220 us
  waiting for transfers between devices  102 us (46%)
  blocking collectives  69.4 us (32%)
  between operations  17.2 us (8%)
  matrix products  12.2 us (6%)
  other arithmetic  11.5 us (5%)
  local copies, waits for them, and re-layouts  7.61 us (3%)
    psum x1, blocking collectives, body(): grads = lax.psum(shard_sum, 'rep')  59.9 us
    reduce_scatter x1, waiting for transfers between devices, body(): lax.psum_scatter(jnp.concatenate([contract_rows(tokens_part, d_qkv), cont...  44.1 us
    all_gather x1, waiting for transfers between devices, body(): lax.all_gather(w_qkv, 'fsdp', axis=0, tiled=True)  34.4 us
    all_gather x1, waiting for transfers between devices, body(): lax.all_gather(w_out_t, 'fsdp', axis=0, tiled=True)  21.9 us
    psum x1, blocking collectives, body(): norm_sq = lax.psum(jnp.sum(grads * grads), 'fsdp')  9.53 us
    unnamed x20, local copies, waits for them, and re-layouts  4.97 us
    dot_general x5, matrix products, contract_cols(): lax.dot_general(left, right, (((1,), (1,)), ((), ())), preferred_element_...  4.91 us
  transfers between devices with their start and end apart: 3, of which 3 were waited for; matrix products, arithmetic and copies ran while one was open for 5% of the time, Pallas kernels for 0%

commit v1 on v0

--- a/solution.py
+++ b/solution.py
@@ -129,7 +129,9 @@
         scatter_dimension=0,
         tiled=True,
     ).astype(jnp.float32)
-    grads = lax.psum(shard_sum, "rep")
+    grads = shard_sum
+    for hop in (1, 2, 4):
+        grads = grads + lax.ppermute(grads, "rep", [(dev, dev ^ hop) for dev in range(8)])
     norm_sq = lax.psum(jnp.sum(grads * grads), "fsdp")
     grad_update = grads * lax.rsqrt(norm_sq / (D * grads.shape[1]) + 1e-06)
     return (input_grad, grad_update, jnp.sqrt(norm_sq))

time: 220 us -> 269 us (1.22)
  waiting for transfers between devices: 102 us -> 206 us
  blocking collectives: 69.4 us -> 9.54 us
  starting transfers between devices: 0.11 us -> 4.21 us
    ppermute x0 -> x3, waiting for transfers between devices: none -> 104 us  [body(): lax.ppermute(grads, 'rep', [(dev, dev ^ hop) for dev in range(8)])]
    psum x1 -> x0, blocking collectives: 59.9 us -> none  [body(): grads = lax.psum(shard_sum, 'rep')]
    ppermute x0 -> x3, starting transfers between devices: none -> 4.09 us  [body(): lax.ppermute(grads, 'rep', [(dev, dev ^ hop) for dev in range(8)])]
  transfers between devices with their start and end apart: 3 -> 6, of which waited for: 3 -> 6; matrix products, arithmetic and copies ran while one was open for 5% -> 5% of each run, Pallas kernels for 0% -> 0%
where the time goes in v1:
time: 269 us
  waiting for transfers between devices  206 us (77%)
  between operations  17.2 us (6%)
  other arithmetic  13.5 us (5%)
  matrix products  10.6 us (4%)
  blocking collectives  9.54 us (4%)
  local copies, waits for them, and re-layouts  7.62 us (3%)
  starting transfers between devices  4.21 us (2%)
    ppermute x3, waiting for transfers between devices, body(): lax.ppermute(grads, 'rep', [(dev, dev ^ hop) for dev in range(8)])  104 us
    reduce_scatter x1, waiting for transfers between devices, body(): lax.psum_scatter(jnp.concatenate([contract_rows(tokens_part, d_qkv), cont...  44.1 us
    all_gather x1, waiting for transfers between devices, body(): lax.all_gather(w_qkv, 'fsdp', axis=0, tiled=True)  34.4 us
    all_gather x1, waiting for transfers between devices, body(): lax.all_gather(w_out_t, 'fsdp', axis=0, tiled=True)  21.9 us
    psum x1, blocking collectives, body(): norm_sq = lax.psum(jnp.sum(grads * grads), 'fsdp')  9.54 us
  transfers between devices with their start and end apart: 6, of which 6 were waited for; matrix products, arithmetic and copies ran while one was open for 5% of the time, Pallas kernels for 0%

profile of v1, /device:TPU:0, one launch (start us, length us, event | category | flops | bytes accessed | tf_op | source)
XLA Modules:
  0.0 268.9 jit_solution(11960649688716689603)
XLA Ops:
  13.2 1.4 fusion.50
  14.6 1.2 broadcast_multiply_fusion.1
  15.8 1.4 convolution_convert_fusion.2
  17.2 21.9 %all-gather.5.cloned.1.call-done = bf16[2048,256]{1,0:T(8,128)(2,1)} async-done(((bf16[512,256]{1,0:T(8,128)(2,1)}), bf16[2048,256]{1,0:T(8,128)(2,1)}) %all-gather.5.cloned.1.call-update) | async-done | bytes 1048592 | tf_op jit(solution)/shard_map/all_gather | solution.py:58
  39.1 1.7 convolution_convert_fusion.3
  40.8 0.9 multiply_reduce_fusion.1
  41.8 34.4 %all-gather.3.cloned.1.call-done = bf16[2048,512]{1,0:T(8,128)(2,1)} async-done(((bf16[512,512]{1,0:T(8,128)(2,1)}), bf16[2048,512]{1,0:T(8,128)(2,1)}) %all-gather.3.cloned.1.call-update) | async-done | bytes 2097168 | tf_op jit(solution)/shard_map/all_gather | solution.py:53
  76.1 2.3 fusion.51
  78.6 0.9 fusion.28
  80.6 1.0 fusion.10
  84.4 1.2 subtract_convert_fusion
  86.7 1.9 pad_maximum_fusion
  88.6 44.1 %reduce-scatter.2.cloned.1.call-done = bf16[512,768]{0,1:T(8,128)(2,1)} async-done(((bf16[2048,768]{0,1:T(8,128)(2,1)}), bf16[512,768]{0,1:T(8,128)(2,1)}) %reduce-scatter.2.cloned.1.call-update) | async-done | bytes 786448 | tf_op jit(solution)/shard_map/reduce_scatter | solution.py:124
  132.7 1.4 convert_element_type.92
  134.2 3.4 %collective-permute-done = f32[512,768]{0,1:T(8,128)S(1)} collective-permute-done((f32[512,768]{0,1:T(8,128)S(1)}, f32[512,768]{0,1:T(8,128)S(1)}, u32[]{:S(2)}, u32[]{:S(2)}) %collective-permute-start) | collective-permute-done | bytes 1572896 | tf_op jit(solution)/shard_map/ppermute | solution.py:134
  137.8 1.6 collective-permute-start.1
  139.4 35.0 %collective-permute-done.1 = f32[512,768]{0,1:T(8,128)S(1)} collective-permute-done((f32[512,768]{0,1:T(8,128)S(1)}, f32[512,768]{0,1:T(8,128)S(1)}, u32[]{:S(2)}, u32[]{:S(2)}) %collective-permute-start.1) | collective-permute-done | bytes 1572896 | tf_op jit(solution)/shard_map/ppermute | solution.py:134
  174.7 2.5 collective-permute-start.2
  177.2 1.7 convolution_convert_fusion.1
  178.9 66.1 %collective-permute-done.2 = f32[512,768]{0,1:T(8,128)S(1)} collective-permute-done((f32[512,768]{0,1:T(8,128)S(1)}, f32[512,768]{0,1:T(8,128)S(1)}, u32[]{:S(2)}, u32[]{:S(2)}) %collective-permute-start.2) | collective-permute-done | bytes 1572896 | tf_op jit(solution)/shard_map/ppermute | solution.py:134
  244.9 1.1 multiply_reduce_fusion
  246.0 9.5 %psum.7 = f32[]{:T(128)} all-reduce(f32[]{:T(128)} %get-tuple-element.56), channel_id=1, replica_groups=mesh['fsdp'=4,'rep'=8] {'fsdp'}, use_global_device_ids=true, to_apply=%region_6.7 | all-reduce | flops 1 | bytes 8 | tf_op jit(solution)/shard_map/psum | solution.py:135
  256.9 1.3 broadcast_multiply_fusion
  258.2 3.0 %copy.34 = f32[512,768]{1,0:T(8,128)} copy(f32[512,768]{0,1:T(8,128)} %broadcast_multiply_fusion) | data formatting | bytes 3145728
  (59 shorter events, 11.0 us)
Async XLA Ops:
  7.2 69.0 %copy-start = (bf16[256,2048]{1,0:T(8,128)(2,1)S(1)}, bf16[256,2048]{1,0:T(8,128)(2,1)}, u32[]{:S(2)}) copy-start(bf16[256,2048]{1,0:T(8,128)(2,1)} %param.8) | copy-start | bytes 3145732
  7.2 8.6 %copy-start.1 = (bf16[256,2048]{1,0:T(8,128)(2,1)S(1)}, bf16[256,2048]{1,0:T(8,128)(2,1)}, u32[]{:S(2)}) copy-start(bf16[256,2048]{1,0:T(8,128)(2,1)} %param.9) | copy-start | bytes 3145732
  7.2 31.9 %all-gather.5.cloned.1.call-start = ((), (), s32[]{:S(2)}) async-start(), calls=%async_computation.2 | async-start | bytes 1310720 | tf_op jit(solution)/shard_map/all_gather | solution.py:58
  7.9 68.2 %all-gather.3.cloned.1.call-start = ((), (), s32[]{:S(2)}) async-start(), calls=%async_computation.1 | async-start | bytes 2621440 | tf_op jit(solution)/shard_map/all_gather | solution.py:53
  8.7 124.0 %reduce-scatter.2.cloned.1.call-start = ((), (), s32[]{:S(2)}) async-start(), calls=%async_computation.3 | async-start | bytes 3932160 | tf_op jit(solution)/shard_map/reduce_scatter | solution.py:124
  79.7 2.3 copy-start.3
  79.7 2.3 copy-start.4
  79.7 2.7 %copy-start.5 = (f32[256,1]{0,1:T(1,128)S(1)}, f32[256,1]{0,1:T(1,128)}, u32[]{:S(2)}) copy-start(f32[256,1]{0,1:T(1,128)} %get-tuple-element.70) | copy-start | bytes 3076
  79.7 2.7 %copy-start.7 = (s32[256]{0:T(256)S(1)}, s32[256]{0:T(256)}, u32[]{:S(2)}) copy-start(s32[256]{0:T(256)} %convert_reduce_fusion) | copy-start | bytes 3076
  132.7 4.9 %copy-start.2 = (bf16[512,768]{0,1:T(8,128)(2,1)S(1)}, bf16[512,768]{0,1:T(8,128)(2,1)}, u32[]{:S(2)}) copy-start(bf16[512,768]{0,1:T(8,128)(2,1)} %reduce-scatter.2.cloned.1.call-done) | copy-start | bytes 2359300
  134.1 3.5 %collective-permute-start = (f32[512,768]{0,1:T(8,128)S(1)}, f32[512,768]{0,1:T(8,128)S(1)}, u32[]{:S(2)}, u32[]{:S(2)}) collective-permute-start(f32[512,768]{0,1:T(8,128)S(1)} %convert_element_type.92), channel_id=1, source_target_pairs={{0,1},{1,0},{2,3},{3,2},{4,5},{5,4},{6,7},{7,6},{8,9},{9,8},{10,11... | collective-permute-start | bytes 4718600 | tf_op jit(solution)/shard_map/ppermute | solution.py:134
  137.8 39.3 %copy-start.6 = (bf16[2048,512]{1,0:T(8,128)(2,1)S(1)}, bf16[2048,512]{1,0:T(8,128)(2,1)}, u32[]{:S(2)}) copy-start(bf16[2048,512]{1,0:T(8,128)(2,1)} %all-gather.3.cloned.1.call-done) | copy-start | bytes 6291460
  137.8 36.5 %collective-permute-start.1 = (f32[512,768]{0,1:T(8,128)S(1)}, f32[512,768]{0,1:T(8,128)S(1)}, u32[]{:S(2)}, u32[]{:S(2)}) collective-permute-start(f32[512,768]{0,1:T(8,128)S(1)} %convert_add_fusion), channel_id=1, source_target_pairs={{0,2},{1,3},{2,0},{3,1},{4,6},{5,7},{6,4},{7,5},{8,10},{9,11},{10,... | collective-permute-start | bytes 4718600 | tf_op jit(solution)/shard_map/ppermute | solution.py:134
  174.7 70.3 %collective-permute-start.2 = (f32[512,768]{0,1:T(8,128)S(1)}, f32[512,768]{0,1:T(8,128)S(1)}, u32[]{:S(2)}, u32[]{:S(2)}) collective-permute-start(f32[512,768]{0,1:T(8,128)S(1)} %add.61), channel_id=1, source_target_pairs={{0,4},{1,5},{2,6},{3,7},{4,0},{5,1},{6,2},{7,3},{8,12},{9,13},{10,... | collective-permute-start | bytes 4718600 | tf_op jit(solution)/shard_map/ppermute | solution.py:134
Sparse Core Ops, SparseCore 0:
  9.8 29.2 all-gather.4
  40.9 35.1 all-gather.2
  88.7 43.8 reduce-scatter.1
